TPU v7x, 32 devices: a whole 2x2x4 slice. The times are simulated.
32 devices in a mesh: events: 2 (over y), blk: 4 (over z), sub: 2 (over x), pair: 2 (over core).
Axes of the slice: x: 2, y: 2, z: 4, core: 2. Of those that a mesh axis runs over, the one named last changes fastest.
Arguments:
- synthetic: bfloat16 [2560, 4096], P(('events', 'sub', 'pair'), 'blk'), parts along dimension 0, may hold values from -6 to 6
- observed: bfloat16 [2560, 4096], P(('events', 'sub', 'pair'), 'blk'), parts along dimension 0, may hold values from -6 to 6
- station_weights: int32 [2560], P('events'), parts along dimension 0, may hold values from 1 to 4
- pair_mask: int32 [32, 16], P('events'), parts along dimension 0, may hold values from 0 to 1, as said below
Outputs:
- adjoint_traces: bfloat16 [2560, 4096], P(('events', 'sub', 'pair'), 'blk'), parts along dimension 0
There are 2 independent parts, one for each index of `events`. A program takes and returns all parts, laid end to end along the dimension named above; each array names one. Nothing has to cross between parts.
Inputs may be any that keep to these rules, and one draw needn't show every extreme that they name: pair_mask[p, q] is 1 where station pieces p and q are coupled; piece p holds stations p * 80 to (p + 1) * 80 - 1.
All inputs are finite; a program needn't handle non-finite values.
Results may differ from a plain program's by a relative error of at most 0.025.
Values may be sent and summed in bfloat16 or wider, within the bound.
No kernel may reach another device: no remote copies, remote signals or barrier semaphores. Data moves between devices by JAX's collectives and lax.ppermute only.
A program may use at most 64 MiB of HBM per device.

v0:
```python
import functools
import math

import jax
import jax.numpy as jnp
from jax import lax
from jax.experimental import pallas as pl
from jax.experimental.pallas import tpu as pltpu
from jax.sharding import PartitionSpec as P


NT = 4096
NF = 512
F_LO = 64

epsilon = 1e-06
CONTRACT_LAST = (((1,), (1,)), ((), ()))
VMEM = pl.BlockSpec(memory_space=pltpu.VMEM)


def shift(value, axis, steps):
    count = lax.axis_size(axis)
    pairs = [(source, (source + steps) % count) for source in range(count)]
    return lax.ppermute(value, axis, pairs)


def sweep(count):
    order = []
    for near in range(1, count // 2 + 1):
        order.append(near)
        if (count - near) % count != near:
            order.append(count - near)
    return order


def cos_sin(samples):
    bins = F_LO + jnp.arange(NF, dtype=jnp.int32)
    phases = samples[:, None] * bins[None, :] % NT
    angles = phases.astype(jnp.float32) * (2.0 * math.pi / NT)
    return jnp.cos(angles), jnp.sin(angles)


def basis_kernel(per_step, low_rows, hc_ref, hs_ref, lc_ref, ls_ref, out_ref):
    step = pl.program_id(0)
    for h in range(per_step):
        hc = hc_ref[pl.ds(step * per_step + h, 1), :]
        hs = hs_ref[pl.ds(step * per_step + h, 1), :]
        lc = lc_ref[...]
        ls = ls_ref[...]
        rows = slice(h * low_rows, (h + 1) * low_rows)
        out_ref[rows, :NF] = (hc * lc - hs * ls).astype(jnp.bfloat16)
        out_ref[rows, NF:] = (-(hs * lc + hc * ls)).astype(jnp.bfloat16)


def make_basis(firsts, span):
    low_rows = math.gcd(span, 64)
    low_c, low_s = cos_sin(jnp.arange(low_rows, dtype=jnp.int32))
    highs = (firsts[:, None] + jnp.arange(0, span, low_rows, dtype=jnp.int32)[None, :]).reshape(-1)
    high_c, high_s = cos_sin(highs)
    per_step = math.gcd(highs.shape[0], 4)
    whole = lambda a: pl.BlockSpec(a.shape, lambda i: (0, 0))
    rows = highs.shape[0] * low_rows
    return pl.pallas_call(
        functools.partial(basis_kernel, per_step, low_rows),
        grid=(highs.shape[0] // per_step,),
        in_specs=[whole(high_c), whole(high_s), whole(low_c), whole(low_s)],
        out_specs=pl.BlockSpec((per_step * low_rows, 2 * NF), lambda i: (i, 0)),
        out_shape=jax.ShapeDtypeStruct((rows, 2 * NF), jnp.bfloat16),
        cost_estimate=pl.CostEstimate(
            flops=8 * rows * NF, bytes_accessed=4 * rows * NF, transcendentals=0
        ),
        compiler_params=pltpu.CompilerParams(vmem_limit_bytes=16 << 20),
        name="basis",
    )(high_c, high_s, low_c, low_s)


def angular_row():
    bins = F_LO + lax.broadcasted_iota(jnp.int32, (1, NF), 1)
    return 2.0 * math.pi / NT * bins.astype(jnp.float32)


def rate_of(re, im):
    angular = angular_row()
    return jnp.concatenate([-angular * im, angular * re], axis=1).astype(jnp.bfloat16)


def tile_kernel(first, rows_ref, power_ref, coef_ref, gain_ref, col_ref, *rest):
    out_ref = rest[-1]
    col = col_ref[...].astype(jnp.float32)
    model_rate = rate_of(col[:, :NF], col[:, NF : 2 * NF])
    data_rate = rate_of(-col[:, 2 * NF : 3 * NF], -col[:, 3 * NF :])
    both = jnp.concatenate([model_rate, data_rate], axis=1)
    cross = lax.dot_general(
        rows_ref[...], both, CONTRACT_LAST, preferred_element_type=jnp.float32
    )
    col_power = lax.dot_general(
        jnp.ones((8, 2 * NF), jnp.float32),
        jnp.square(model_rate.astype(jnp.float32)),
        CONTRACT_LAST,
        precision=lax.Precision.HIGHEST,
        preferred_element_type=jnp.float32,
    )[0:1, :]
    normalizer = 0.5 * (power_ref[...] + col_power) + epsilon
    coupling = (coef_ref[...] * gain_ref[...] * cross / normalizer).astype(jnp.bfloat16)
    update = jnp.dot(coupling, model_rate, preferred_element_type=jnp.float32)
    if first:
        out_ref[...] = update
    else:
        out_ref[...] = rest[0][...] + update


def pair_tile(running, rows, row_power, coef, gain, col):
    args = [rows, row_power, coef, gain, col]
    aliases = {}
    if running is not None:
        aliases = {len(args): 0}
        args.append(running)
    height, width = rows.shape[0], col.shape[0]
    return pl.pallas_call(
        functools.partial(tile_kernel, running is None),
        in_specs=[pl.BlockSpec(memory_space=pltpu.VMEM)] * len(args),
        out_specs=pl.BlockSpec(memory_space=pltpu.VMEM),
        out_shape=jax.ShapeDtypeStruct((height, 2 * NF), jnp.float32),
        input_output_aliases=aliases,
        cost_estimate=pl.CostEstimate(
            flops=12 * height * width * NF,
            bytes_accessed=16 * height * NF,
            transcendentals=0,
        ),
        name="pair_tile",
    )(*args)


def ring_body(synthetic, observed, station_weights, pair_mask):
    levels = lax.axis_size("blk")
    subs = lax.axis_size("sub")
    pairs = lax.axis_size("pair")
    level = lax.axis_index("blk")
    sub = lax.axis_index("sub")
    pair = lax.axis_index("pair")
    span = synthetic.shape[1]
    piece = synthetic.shape[0] // levels
    stations = station_weights.shape[0]

    def owned_by(steps):
        owner = (level + steps) % levels
        return jnp.concatenate(
            [
                lax.dynamic_slice_in_dim(synthetic, owner * piece, piece, 0),
                lax.dynamic_slice_in_dim(observed, owner * piece, piece, 0),
            ],
            axis=0,
        )

    order = sweep(levels)
    blocks = {0: owned_by(0)}
    for steps in order:
        blocks[steps] = shift(owned_by(steps), "blk", steps)
    arrivals = [0] + order
    firsts = jnp.stack([(level - steps) % levels * span for steps in arrivals]).astype(jnp.int32)
    basis = make_basis(firsts, span)
    member = sub * pairs + pair
    members = jnp.stack(
        [
            (sub - s) % subs * pairs + (pair - q) % pairs
            for s in range(subs)
            for q in range(pairs)
        ]
    )
    gains = station_weights.astype(jnp.float32).reshape(-1, piece)
    link = jnp.maximum(pair_mask, pair_mask.T).astype(jnp.float32)
    row_pieces = members * levels + level
    row_gain = gains[row_pieces].reshape(-1, 1)
    row_link = link[row_pieces]
    factor = 4.0 / math.sqrt(stations)
    coefs, col_gains = [], []
    for steps in arrivals:
        column_piece = member * levels + (level - steps) % levels
        active = lax.dynamic_slice_in_dim(row_link, column_piece, 1, 1)
        coefs.append(factor * row_gain * jnp.repeat(active, piece, axis=0))
        col_gains.append(lax.dynamic_slice_in_dim(gains, column_piece, 1, 0))
    last = order[-1]
    blocks[last], coefs, col_gains = lax.optimization_barrier((blocks[last], coefs, col_gains))
    total = None
    for place, steps in enumerate(arrivals):
        part = jnp.dot(
            blocks[steps],
            basis[place * span : (place + 1) * span],
            preferred_element_type=jnp.float32,
        )
        total = part if total is None else total + part
    spec = (total * (1.0 / math.sqrt(NT))).astype(jnp.bfloat16)
    own = jnp.concatenate([spec[:piece], spec[piece:]], axis=1)

    columns = {0: own}
    for steps in order:
        columns[steps] = shift(own, "blk", steps)
    blocks_of_rows = []
    for s in range(subs):
        here = own if s == 0 else shift(own, "sub", s)
        for q in range(pairs):
            blocks_of_rows.append(here if q == 0 else shift(here, "pair", q))
    rows = jnp.concatenate(blocks_of_rows, axis=0)
    widened = rows[:, : 2 * NF].astype(jnp.float32)
    row_rate = rate_of(widened[:, :NF], widened[:, NF:])
    row_power = jnp.sum(jnp.square(row_rate.astype(jnp.float32)), axis=1, keepdims=True)

    running = None
    for place, steps in enumerate(arrivals):
        running = pair_tile(
            running, rows, row_power, coefs[place], col_gains[place], columns[steps]
        )

    partial = running.reshape(subs, pairs, piece, 2 * NF)
    held = partial[:, 0]
    for q in range(1, pairs):
        sent = partial[:, q].astype(jnp.bfloat16)
        held = held + shift(sent, "pair", -q).astype(jnp.float32)
    adjoint = held[0]
    for s in range(1, subs):
        adjoint = adjoint + shift(held[s].astype(jnp.bfloat16), "sub", -s).astype(jnp.float32)
    adjoint = adjoint.astype(jnp.bfloat16)

    gathered = jnp.zeros((levels * piece, 2 * NF), jnp.bfloat16)
    for steps in arrivals:
        arrived = adjoint if steps == 0 else shift(adjoint, "blk", steps)
        gathered = lax.dynamic_update_slice_in_dim(
            gathered, arrived, (level - steps) % levels * piece, 0
        )
    return (
        lax.dot_general(
            gathered, basis[:span], CONTRACT_LAST, preferred_element_type=jnp.float32
        )
        * (1.0 / math.sqrt(NF))
    ).astype(jnp.bfloat16)


def power_of(spec):
    wide = spec.astype(jnp.float32)
    rate = rate_of(wide[:, :NF], wide[:, NF:])
    return rate, jnp.sum(jnp.square(rate.astype(jnp.float32)), axis=1, keepdims=True)


def couple_kernel(piece, row_count, col_count, before, out_count, *refs):
    row_refs = refs[:row_count]
    col_refs = refs[row_count : row_count + col_count]
    gain_ref, weight_ref = refs[-out_count - 2 : -out_count]
    sums = row_count // (gain_ref.shape[1] // piece)
    row_models, row_datas = [], []
    for at in range(0, row_count, sums):
        block = row_refs[at][...]
        if sums == 2:
            block = (
                block.astype(jnp.float32) + row_refs[at + 1][...].astype(jnp.float32)
            ).astype(jnp.bfloat16)
        row_models.append(block[:piece])
        row_datas.append(block[piece:])
    row_model = jnp.concatenate(row_models, axis=0)
    row_data = jnp.concatenate(row_datas, axis=0)
    row_power = power_of(row_model)[1]
    models, datas, powers = [], [], []
    for ref in col_refs:
        rate, power = power_of(ref[:piece])
        models.append(rate)
        powers.append(power)
        wide = ref[piece:].astype(jnp.float32)
        datas.append(rate_of(wide[:, :NF], wide[:, NF:]))
    col_model = jnp.concatenate(models, axis=0)
    col_data = jnp.concatenate(datas, axis=0)
    powers = jnp.concatenate(powers, axis=0)

    def diagonal(width):
        return lax.broadcasted_iota(jnp.int32, (width, width), 0) == lax.broadcasted_iota(
            jnp.int32, (width, width), 1
        )

    col_power = jnp.sum(
        jnp.where(diagonal(powers.shape[0]), powers, 0.0), axis=0, keepdims=True
    )
    height = gain_ref.shape[1]
    row_gain = jnp.sum(
        jnp.where(diagonal(height), gain_ref[...], 0.0), axis=1, keepdims=True
    )
    cross = lax.dot_general(
        row_model, col_model, CONTRACT_LAST, preferred_element_type=jnp.float32
    ) - lax.dot_general(row_data, col_data, CONTRACT_LAST, preferred_element_type=jnp.float32)
    normalizer = 0.5 * (row_power + col_power) + epsilon
    ratio = row_gain * cross / normalizer
    coupling = jnp.concatenate(
        [
            (weight_ref[at : at + 1, :] * ratio[at * piece : (at + 1) * piece]).astype(
                jnp.bfloat16
            )
            for at in range(height // piece)
        ],
        axis=0,
    )
    update = jnp.dot(coupling, col_model, preferred_element_type=jnp.float32)
    if before:
        update = update + refs[row_count + col_count][...]
    for place, out_ref in enumerate(refs[-out_count:]):
        rows = out_ref.shape[0]
        out_ref[...] = update[place * rows : (place + 1) * rows].astype(out_ref.dtype)


def couple(rows, cols, gains, weights, piece, outs, before=None, kind=jnp.bfloat16):
    args = [*rows, *cols] + ([] if before is None else [before]) + [gains, weights]
    height, width = gains.shape[1], weights.shape[1]
    return pl.pallas_call(
        functools.partial(
            couple_kernel, piece, len(rows), len(cols), before is not None, outs
        ),
        in_specs=[VMEM] * len(args),
        out_specs=[VMEM] * outs,
        out_shape=[jax.ShapeDtypeStruct((height // outs, 2 * NF), kind)] * outs,
        compiler_params=pltpu.CompilerParams(vmem_limit_bytes=16 << 20),
        cost_estimate=pl.CostEstimate(
            flops=12 * height * width * NF,
            bytes_accessed=8 * (height + width) * NF,
            transcendentals=0,
        ),
        name="couple",
    )(*args)


def to_time_kernel(count, own_side, *refs):
    basis_ref = refs[2 * count]
    out_ref, stage_ref, done_sem = refs[-3:]
    level = lax.axis_index("blk")
    is_inner = (level == 1) | (level == 2)
    upper = level >= 2
    block = jnp.where(upper, 1, 0) if own_side else jnp.where(upper, 0, 1)
    adjoint = jnp.concatenate(
        [
            jnp.where(is_inner, here_ref[...], there_ref[...])
            for here_ref, there_ref in zip(refs[:count], refs[count : 2 * count])
        ],
        axis=0,
    )
    half, span = stage_ref.shape
    start = pl.multiple_of(block * half, half)
    wide = span // 2
    copies = []
    for part in range(2):
        columns = slice(part * wide, (part + 1) * wide)
        traces = lax.dot_general(
            adjoint, basis_ref[columns, :], CONTRACT_LAST, preferred_element_type=jnp.float32
        )
        stage_ref[:, columns] = (traces * (1.0 / math.sqrt(NF))).astype(jnp.bfloat16)
        copies.append(
            pltpu.make_async_copy(
                stage_ref.at[:, columns],
                out_ref.at[pl.ds(start, half), columns],
                done_sem.at[part],
            )
        )
        copies[-1].start()
    for copy in copies:
        copy.wait()


def to_time(own_side, here, there, basis, rows, before):
    span = basis.shape[0]
    half = sum(block.shape[0] for block in here)
    args = [*here, *there, basis]
    specs = [VMEM] * len(args)
    aliases = {}
    if before is not None:
        aliases = {len(args): 0}
        specs.append(pl.BlockSpec(memory_space=pl.ANY))
        args.append(before)
    return pl.pallas_call(
        functools.partial(to_time_kernel, len(here), own_side),
        in_specs=specs,
        out_specs=pl.BlockSpec(memory_space=pl.ANY),
        out_shape=jax.ShapeDtypeStruct((rows, span), jnp.bfloat16),
        scratch_shapes=[
            pltpu.VMEM((half, span), jnp.bfloat16),
            pltpu.SemaphoreType.DMA((2,)),
        ],
        input_output_aliases=aliases,
        compiler_params=pltpu.CompilerParams(vmem_limit_bytes=12 << 20),
        cost_estimate=pl.CostEstimate(
            flops=4 * half * span * NF, bytes_accessed=4 * span * NF, transcendentals=0
        ),
        name="to_time",
    )(*args)


def two_bases_kernel(per_step, low_rows, *refs):
    lc_ref, ls_ref = refs[4:6]
    for high, out_ref in zip((refs[:2], refs[2:4]), refs[6:]):
        basis_kernel(per_step, low_rows, *high, lc_ref, ls_ref, out_ref)


def two_bases(first, second, span):
    low_rows = math.gcd(span, 64)
    tables = []
    for start in (first, second):
        tables += cos_sin(start + jnp.arange(0, span, low_rows, dtype=jnp.int32))
    tables += cos_sin(jnp.arange(low_rows, dtype=jnp.int32))
    per_step = math.gcd(span // low_rows, 4)
    block = pl.BlockSpec((per_step * low_rows, 2 * NF), lambda i: (i, 0))
    return pl.pallas_call(
        functools.partial(two_bases_kernel, per_step, low_rows),
        grid=(span // low_rows // per_step,),
        in_specs=[pl.BlockSpec(table.shape, lambda i: (0, 0)) for table in tables],
        out_specs=[block, block],
        out_shape=[jax.ShapeDtypeStruct((span, 2 * NF), jnp.bfloat16)] * 2,
        compiler_params=pltpu.CompilerParams(vmem_limit_bytes=12 << 20),
        cost_estimate=pl.CostEstimate(
            flops=16 * span * NF, bytes_accessed=8 * span * NF, transcendentals=0
        ),
        name="two_bases",
    )(*tables)


def own_parts_kernel(count, *refs):
    basis_ref = refs[count]
    for block_ref, out_ref in zip(refs[:count], refs[count + 1 :]):
        out_ref[...] = jnp.dot(
            block_ref[...], basis_ref[...], preferred_element_type=jnp.float32
        )


def own_parts(blocks, basis):
    rows, span = blocks[0].shape
    return pl.pallas_call(
        functools.partial(own_parts_kernel, len(blocks)),
        in_specs=[VMEM] * (len(blocks) + 1),
        out_specs=[VMEM] * len(blocks),
        out_shape=[jax.ShapeDtypeStruct((rows, 2 * NF), jnp.float32)] * len(blocks),
        compiler_params=pltpu.CompilerParams(vmem_limit_bytes=12 << 20),
        cost_estimate=pl.CostEstimate(
            flops=4 * len(blocks) * rows * span * NF,
            bytes_accessed=4 * span * NF,
            transcendentals=0,
        ),
        name="own_parts",
    )(*blocks, basis)


def sum_kernel(part_ref, near_ref, basis_ref, *rest):
    total = part_ref[...] + jnp.dot(
        near_ref[...], basis_ref[...], preferred_element_type=jnp.float32
    )
    total = total * (1.0 / math.sqrt(NT))
    if len(rest) == 3:
        rest_ref, own_ref, sum_ref = rest
        own_ref[...] = (total + rest_ref[...].astype(jnp.float32)).astype(jnp.bfloat16)
    else:
        sum_ref = rest[0]
    sum_ref[...] = total.astype(jnp.bfloat16)


def spectra(part, near, basis, others=None):
    rows, span = near.shape
    args = [part, near, basis] + ([] if others is None else [others])
    outs = 1 if others is None else 2
    return pl.pallas_call(
        sum_kernel,
        in_specs=[VMEM] * len(args),
        out_specs=[VMEM] * outs,
        out_shape=[jax.ShapeDtypeStruct((rows, 2 * NF), jnp.bfloat16)] * outs,
        compiler_params=pltpu.CompilerParams(vmem_limit_bytes=12 << 20),
        cost_estimate=pl.CostEstimate(
            flops=4 * rows * span * NF, bytes_accessed=4 * span * NF, transcendentals=0
        ),
        name="spectra",
    )(*args)


def inner_body(synthetic, observed, station_weights, pair_mask):
    levels = lax.axis_size("blk")
    subs = lax.axis_size("sub")
    pairs = lax.axis_size("pair")
    level = lax.axis_index("blk")
    sub = lax.axis_index("sub")
    pair = lax.axis_index("pair")
    span = synthetic.shape[1]
    half = synthetic.shape[0] // 2
    per_half = levels // 2
    stations = station_weights.shape[0]
    piece = half // per_half
    side = level // 2
    inward, swapped, outward = [(0, 1), (3, 2)], [(1, 2), (2, 1)], [(1, 0), (2, 3)]

    def piece_of(which, at, sources):
        return jnp.concatenate(
            [
                lax.dynamic_slice_in_dim(source, which * half + at, piece, 0)
                for source in sources
            ],
            axis=0,
        )

    sources = (synthetic, observed)
    front = piece_of(1 - side, 0, sources)
    front, sources = lax.optimization_barrier((front, sources))
    passed = [front] + [piece_of(1 - side, at, sources) for at in range(piece, half, piece)]
    kept = [piece_of(side, at, sources) for at in range(0, half, piece)]
    near_passed, near_kept = [], []
    for blocks, arrived in ((passed, near_passed), (kept, near_kept)):
        for block in blocks:
            arrived.append(lax.ppermute(block, "blk", inward))

    member = sub * pairs + pair
    hops = [(s, q) for s in range(subs) for q in range(pairs)]
    starts = [
        ((sub - s) % subs * pairs + (pair - q) % pairs) * 2 * half + side * half + at
        for at in range(0, half, piece)
        for s, q in hops
    ]
    gains = station_weights.astype(jnp.float32)
    col_gains = jnp.concatenate(
        [lax.dynamic_slice_in_dim(gains, start, piece, 0) for start in starts]
    )[None, :]
    firsts = [member * 2 * half + which * half for which in (side, 1 - side)]
    own_gains, other_gains = [
        lax.dynamic_slice_in_dim(gains, start, half, 0)[None, :] for start in firsts
    ]
    link = jnp.maximum(pair_mask, pair_mask.T).astype(jnp.float32)
    link_rows = jnp.concatenate(
        [lax.dynamic_slice_in_dim(link, start // piece, per_half, 0) for start in firsts], axis=0
    )
    col_pieces = jnp.repeat(jnp.stack(starts) // piece, piece)
    chosen = jnp.arange(link.shape[0], dtype=jnp.int32)[:, None] == col_pieces[None, :]
    active = jnp.sum(jnp.where(chosen[None], link_rows[:, :, None], 0.0), axis=1)
    weights = 4.0 / math.sqrt(stations) * col_gains * active
    late = (subs - 1) * pairs
    early_width = (len(starts) - late) * piece
    own_early, own_late = weights[:per_half, :early_width], weights[:per_half, early_width:]
    here, own_gains, other_gains, own_early, own_late, other_weights = lax.optimization_barrier(
        (level, own_gains, other_gains, own_early, own_late, weights[per_half:])
    )

    here_basis, near_basis = two_bases(here * span, (here ^ 1) * span, span)
    passed_parts = own_parts(passed, here_basis)
    kept_parts = own_parts(kept, here_basis)
    to_pass, kept_rest = [], []
    for place in range(per_half):
        (summed,) = spectra(passed_parts[place], near_passed[place], near_basis)
        to_pass.append(summed)
        kept_rest.append(lax.ppermute(summed, "blk", swapped))
    own, passed_rest, cols = [], [], {}
    for place in range(per_half):
        whole, summed = spectra(
            kept_parts[place], near_kept[place], near_basis, kept_rest[place]
        )
        own.append(whole)
        for s, q in hops:
            if q == 0:
                cols[s, q, place] = whole if s == 0 else shift(whole, "sub", s)
            else:
                cols[s, q, place] = shift(cols[s, 0, place], "pair", q)
        passed_rest.append(lax.ppermute(summed, "blk", swapped))
    cols = [cols[s, q, place] for place in range(per_half) for s, q in hops]
    (begun,) = couple(own, cols[:-late], own_gains, own_early, piece, 1, None, jnp.float32)
    own_part = couple(own, cols[-late:], own_gains, own_late, piece, per_half, begun)
    other = [block for both in zip(to_pass, passed_rest) for block in both]
    other_part = couple(other, cols, other_gains, other_weights, piece, per_half)

    def finish(sent, mine):
        sums, arrived = [], []
        for place in range(per_half):
            rest = lax.ppermute(sent[place], "blk", swapped)
            whole = mine[place].astype(jnp.float32) + rest.astype(jnp.float32)
            sums.append(whole.astype(jnp.bfloat16))
            arrived.append(lax.ppermute(sums[-1], "blk", outward))
        return sums, arrived

    first = finish(own_part, other_part)
    second = finish(other_part, own_part)
    rows = synthetic.shape[0]
    traces = to_time(False, *first, here_basis, rows, None)
    return to_time(True, *second, here_basis, rows, traces)


def shards(*args):
    body = inner_body if lax.axis_size("blk") == 4 else ring_body
    return body(*args)


def solution(mesh):
    placed = (
        P(("events", "sub", "pair"), "blk"),
        P(("events", "sub", "pair"), "blk"),
        P("events"),
        P("events", None),
    )
    return jax.shard_map(
        shards,
        mesh=mesh,
        in_specs=placed,
        out_specs=P(("events", "sub", "pair"), "blk"),
        check_vma=False,
    )
```

profile of v0, /device:TPU:0, one launch (start us, length us, event | category | flops | bytes accessed | tf_op | source)
XLA Modules:
  0.0 87.9 jit_solution(13899905239812570670)
XLA Ops:
  0.0 1.1 %constant_dynamic-slice_fusion.8 = (bf16[80,1024]{1,0:T(8,128)(2,1)S(1)}, bf16[80,1024]{1,0:T(8,128)(2,1)S(1)}) fusion(bf16[320,1024]{1,0:T(8,128)(2,1)} %param.5, s32[]{:T(128)S(6)} %select_n.133, bf16[320,1024]{1,0:T(8,128)(2,1)} %param.4), kind=kLoop, calls=%fused_computation.52 | loop fusion | bytes 655364 | tf_op jit(solution)/shard_map/dynamic_slice | solution.py:491
  1.1 0.0 copy-start.2
  1.1 0.0 copy-start.1
  1.1 5.0 %collective-permute-start.1 = (bf16[160,1024]{1,0:T(8,128)(2,1)S(1)}, bf16[160,1024]{1,0:T(8,128)(2,1)S(1)}, u32[]{:S(2)}, u32[]{:S(2)}) collective-permute-start(bf16[160,1024]{1,0:T(8,128)(2,1)S(1)} %pad_maximum_fusion.refs_0_), channel_id=1, source_target_pairs={{0,4},{12,8},{1,5},{13,9},{2,6},{14,10},{3,7},{15,11},{16,20},{28,... | collective-permute-start | bytes 983048 | tf_op jit(solution)/shard_map/ppermute | solution.py:505
  6.2 1.1 %constant_dynamic-slice_fusion.5 = (bf16[80,1024]{1,0:T(8,128)(2,1)S(1)}, bf16[80,1024]{1,0:T(8,128)(2,1)S(1)}, bf16[80,1024]{1,0:T(8,128)(2,1)S(1)}) fusion(bf16[320,1024]{1,0:T(8,128)(2,1)} %param.4, s32[]{:T(128)S(6)} %select_n.135, s32[]{:T(128)S(6)} %select_n.159, s32[]{:T(128)S(6)} %select_n.134), kind=kLoop, calls=%fused_computation.49 | loop fusion | bytes 983052 | tf_op jit(solution)/shard_map/dynamic_slice | solution.py:491
  7.4 1.3 %collective-permute-start = (bf16[160,1024]{1,0:T(8,128)(2,1)S(1)}, bf16[160,1024]{1,0:T(8,128)(2,1)S(1)}, u32[]{:S(2)}, u32[]{:S(2)}) collective-permute-start(bf16[160,1024]{1,0:T(8,128)(2,1)S(1)} %pad_maximum_fusion.1.refs_0_), channel_id=1, source_target_pairs={{0,4},{12,8},{1,5},{13,9},{2,6},{14,10},{3,7},{15,11},{16,20},{28,... | collective-permute-start | bytes 983048 | tf_op jit(solution)/shard_map/ppermute | solution.py:505
  8.7 1.3 %collective-permute-start.4 = (bf16[160,1024]{1,0:T(8,128)(2,1)S(1)}, bf16[160,1024]{1,0:T(8,128)(2,1)S(1)}, u32[]{:S(2)}, u32[]{:S(2)}) collective-permute-start(bf16[160,1024]{1,0:T(8,128)(2,1)S(1)} %pad_maximum_fusion.3.refs_1_), channel_id=1, source_target_pairs={{0,4},{12,8},{1,5},{13,9},{2,6},{14,10},{3,7},{15,11},{16,20},{28,... | collective-permute-start | bytes 983048 | tf_op jit(solution)/shard_map/ppermute | solution.py:505
  10.2 0.1 stack.35
  10.3 0.1 broadcast_in_dim.41
  10.4 0.1 eq.42
  10.5 0.1 fusion.21
  10.7 0.1 concatenate.25
  10.8 0.1 copy.7
  10.9 0.1 select_reduce_fusion
  11.0 0.1 slice.13.refs_6_
  11.1 0.1 fusion.22
  11.2 0.5 fusion.6
  11.7 0.3 fusion.14
  12.0 1.2 %two_bases.1 = (bf16[1024,1024]{1,0:T(8,128)(2,1)S(1)}, bf16[1024,1024]{1,0:T(8,128)(2,1)S(1)}) custom-call(f32[16,512]{1,0:T(8,128)S(1)} %get-tuple-element.75.refs_0_, f32[16,512]{1,0:T(8,128)S(1)} %get-tuple-element.76.refs_1_, f32[16,512]{1,0:T(8,128)S(1)} %get-tuple-element.70.refs_2_, f32[16,512]{1,0:T(8,128)S(1)} %get-tuple-element.69.refs_3_, ...), custom_call_target="tpu_custom_call" | custom-call | flops 8388608 | bytes 4194304 | tf_op jit(solution)/shard_map/two_bases/pallas_call | solution.py:404
  13.3 0.9 own_parts.3
  14.1 0.1 collective-permute-done.1.near_ref
  14.2 0.5 spectra.4.refs_0_
  14.7 0.7 collective-permute-start.2
  15.4 7.2 %collective-permute-start.3 = (bf16[160,1024]{1,0:T(8,128)(2,1)S(1)}, bf16[160,1024]{1,0:T(8,128)(2,1)S(1)}, u32[]{:S(2)}, u32[]{:S(2)}) collective-permute-start(bf16[160,1024]{1,0:T(8,128)(2,1)S(1)} %pad_maximum_fusion.2.refs_1_), channel_id=1, source_target_pairs={{0,4},{12,8},{1,5},{13,9},{2,6},{14,10},{3,7},{15,11},{16,20},{28,... | collective-permute-start | bytes 983048 | tf_op jit(solution)/shard_map/ppermute | solution.py:505
  22.6 5.6 %collective-permute-done.4.near_ref = bf16[160,1024]{1,0:T(8,128)(2,1)S(1)} collective-permute-done((bf16[160,1024]{1,0:T(8,128)(2,1)S(1)}, bf16[160,1024]{1,0:T(8,128)(2,1)S(1)}, u32[]{:S(2)}, u32[]{:S(2)}) %collective-permute-start.4) | collective-permute-done | bytes 327712 | tf_op jit(solution)/shard_map/ppermute | solution.py:505
  28.2 0.5 spectra.6.refs_2_
  28.8 0.7 collective-permute-start.5
  29.4 0.9 own_parts.2
  30.3 0.0 collective-permute-done.near_ref
  30.3 0.0 collective-permute-done.2.rest_0_
  30.3 0.5 spectra.5
  30.9 0.7 collective-permute-start.12
  31.6 1.5 %collective-permute-start.9 = (bf16[160,1024]{1,0:T(8,128)(2,1)S(1)}, bf16[160,1024]{1,0:T(8,128)(2,1)S(1)}, u32[]{:S(2)}, u32[]{:S(2)}) collective-permute-start(bf16[160,1024]{1,0:T(8,128)(2,1)S(1)} %get-tuple-element.36.refs_0_.refs_2_.refs_4_), channel_id=1, source_target_pairs={{0,2},{2,0},{1,3},{3,1},{4,6},{6,4},{5,7},{7,5},{8,10},{10,8},{9,1... | collective-permute-start | bytes 983048 | tf_op jit(solution)/shard_map/ppermute | solution.py:24
  33.1 1.0 %collective-permute-done.3.near_ref = bf16[160,1024]{1,0:T(8,128)(2,1)S(1)} collective-permute-done((bf16[160,1024]{1,0:T(8,128)(2,1)S(1)}, bf16[160,1024]{1,0:T(8,128)(2,1)S(1)}, u32[]{:S(2)}, u32[]{:S(2)}) %collective-permute-start.3) | collective-permute-done | bytes 327712 | tf_op jit(solution)/shard_map/ppermute | solution.py:505
  34.1 0.6 spectra.7
  34.7 1.5 %collective-permute-start.6 = (bf16[160,1024]{1,0:T(8,128)(2,1)S(1)}, bf16[160,1024]{1,0:T(8,128)(2,1)S(1)}, u32[]{:S(2)}, u32[]{:S(2)}) collective-permute-start(bf16[160,1024]{1,0:T(8,128)(2,1)S(1)} %get-tuple-element.39.refs_1_.refs_6_.refs_8_), channel_id=1, source_target_pairs={{0,2},{2,0},{1,3},{3,1},{4,6},{6,4},{5,7},{7,5},{8,10},{10,8},{9,1... | collective-permute-start | bytes 983048 | tf_op jit(solution)/shard_map/ppermute | solution.py:24
  36.2 0.0 collective-permute-start.8
  36.2 0.5 collective-permute-start.11
  36.7 0.7 collective-permute-start.13
  37.4 4.5 %collective-permute-done.9.refs_4_.refs_6_ = bf16[160,1024]{1,0:T(8,128)(2,1)S(1)} collective-permute-done((bf16[160,1024]{1,0:T(8,128)(2,1)S(1)}, bf16[160,1024]{1,0:T(8,128)(2,1)S(1)}, u32[]{:S(2)}, u32[]{:S(2)}) %collective-permute-start.9) | collective-permute-done | bytes 327712 | tf_op jit(solution)/shard_map/ppermute | solution.py:24
  41.9 4.2 %collective-permute-done.6.refs_2_.refs_10_ = bf16[160,1024]{1,0:T(8,128)(2,1)S(1)} collective-permute-done((bf16[160,1024]{1,0:T(8,128)(2,1)S(1)}, bf16[160,1024]{1,0:T(8,128)(2,1)S(1)}, u32[]{:S(2)}, u32[]{:S(2)}) %collective-permute-start.6) | collective-permute-done | bytes 327712 | tf_op jit(solution)/shard_map/ppermute | solution.py:24
  46.1 0.0 collective-permute-start.7
  46.1 0.0 collective-permute-done.8.refs_3_.refs_5_
  46.1 0.0 collective-permute-done.13.refs_3_
  46.2 0.0 collective-permute-done.11.refs_7_.refs_9_
  46.2 0.0 collective-permute-done.10.refs_5_.refs_7_
  46.2 1.6 %collective-permute-done.7.refs_3_.refs_11_ = bf16[160,1024]{1,0:T(8,128)(2,1)S(1)} collective-permute-done((bf16[160,1024]{1,0:T(8,128)(2,1)S(1)}, bf16[160,1024]{1,0:T(8,128)(2,1)S(1)}, u32[]{:S(2)}, u32[]{:S(2)}) %collective-permute-start.7) | collective-permute-done | bytes 327712 | tf_op jit(solution)/shard_map/ppermute | solution.py:24
  47.8 1.5 %couple.5 = (bf16[80,1024]{1,0:T(8,128)(2,1)S(1)}, bf16[80,1024]{1,0:T(8,128)(2,1)S(1)}) custom-call(bf16[160,1024]{1,0:T(8,128)(2,1)S(1)} %spectra.4.refs_0_, bf16[160,1024]{1,0:T(8,128)(2,1)S(1)} %collective-permute-done.12.refs_1_, bf16[160,1024]{1,0:T(8,128)(2,1)S(1)} %spectra.6.refs_2_, bf16[160,1024]{1,0:T(8,128)(2,1)S(1)} %collective-permute-done.13.refs_3_, ...), custom_call_target="tpu_custom_call" | custom-call | flops 629145600 | bytes 3276800 | tf_op jit(solution)/shard_map/couple/pallas_call | solution.py:309
  49.3 0.7 collective-permute-start.14
  49.9 0.7 collective-permute-start.15
  50.6 1.2 %couple.3.refs_4_ = f32[160,1024]{1,0:T(8,128)S(1)} custom-call(bf16[160,1024]{1,0:T(8,128)(2,1)S(1)} %get-tuple-element.36.refs_0_.refs_2_.refs_4_, bf16[160,1024]{1,0:T(8,128)(2,1)S(1)} %get-tuple-element.39.refs_1_.refs_6_.refs_8_, bf16[160,1024]{1,0:T(8,128)(2,1)S(1)} %get-tuple-element.36.refs_0_.refs_2_.refs_4_, ...), custom_call_target="tpu_custom_call" | custom-call | flops 471859200 | bytes 2621440 | tf_op jit(solution)/shard_map/couple/pallas_call | solution.py:309
  51.8 0.7 couple.4
  52.5 0.7 collective-permute-start.18
  53.2 0.7 collective-permute-start.19
  53.9 1.3 %collective-permute-start.16 = (bf16[80,1024]{1,0:T(8,128)(2,1)S(1)}, bf16[80,1024]{1,0:T(8,128)(2,1)S(1)}, u32[]{:S(2)}, u32[]{:S(2)}) collective-permute-start(bf16[80,1024]{1,0:T(8,128)(2,1)S(1)} %add_convert_fusion.3.refs_0_), channel_id=1, source_target_pairs={{4,0},{8,12},{5,1},{9,13},{6,2},{10,14},{7,3},{11,15},{20,16},{24,... | collective-permute-start | bytes 491528 | tf_op jit(solution)/shard_map/ppermute | solution.py:569
  55.3 1.3 %collective-permute-start.20 = (bf16[80,1024]{1,0:T(8,128)(2,1)S(1)}, bf16[80,1024]{1,0:T(8,128)(2,1)S(1)}, u32[]{:S(2)}, u32[]{:S(2)}) collective-permute-start(bf16[80,1024]{1,0:T(8,128)(2,1)S(1)} %add_convert_fusion.1.refs_0_), channel_id=1, source_target_pairs={{4,0},{8,12},{5,1},{9,13},{6,2},{10,14},{7,3},{11,15},{20,16},{24,... | collective-permute-start | bytes 491528 | tf_op jit(solution)/shard_map/ppermute | solution.py:569
  56.7 1.3 %collective-permute-start.21 = (bf16[80,1024]{1,0:T(8,128)(2,1)S(1)}, bf16[80,1024]{1,0:T(8,128)(2,1)S(1)}, u32[]{:S(2)}, u32[]{:S(2)}) collective-permute-start(bf16[80,1024]{1,0:T(8,128)(2,1)S(1)} %add_convert_fusion.refs_1_), channel_id=1, source_target_pairs={{4,0},{8,12},{5,1},{9,13},{6,2},{10,14},{7,3},{11,15},{20,16},{24,... | collective-permute-start | bytes 491528 | tf_op jit(solution)/shard_map/ppermute | solution.py:569
  58.0 1.3 %collective-permute-start.17 = (bf16[80,1024]{1,0:T(8,128)(2,1)S(1)}, bf16[80,1024]{1,0:T(8,128)(2,1)S(1)}, u32[]{:S(2)}, u32[]{:S(2)}) collective-permute-start(bf16[80,1024]{1,0:T(8,128)(2,1)S(1)} %add_convert_fusion.2.refs_1_), channel_id=1, source_target_pairs={{4,0},{8,12},{5,1},{9,13},{6,2},{10,14},{7,3},{11,15},{20,16},{24,... | collective-permute-start | bytes 491528 | tf_op jit(solution)/shard_map/ppermute | solution.py:569
  59.3 22.6 %collective-permute-done.20.refs_2_ = bf16[80,1024]{1,0:T(8,128)(2,1)S(1)} collective-permute-done((bf16[80,1024]{1,0:T(8,128)(2,1)S(1)}, bf16[80,1024]{1,0:T(8,128)(2,1)S(1)}, u32[]{:S(2)}, u32[]{:S(2)}) %collective-permute-start.20) | collective-permute-done | bytes 163872 | tf_op jit(solution)/shard_map/ppermute | solution.py:569
  82.0 2.6 %collective-permute-done.21.refs_3_ = bf16[80,1024]{1,0:T(8,128)(2,1)S(1)} collective-permute-done((bf16[80,1024]{1,0:T(8,128)(2,1)S(1)}, bf16[80,1024]{1,0:T(8,128)(2,1)S(1)}, u32[]{:S(2)}, u32[]{:S(2)}) %collective-permute-start.21) | collective-permute-done | bytes 163872 | tf_op jit(solution)/shard_map/ppermute | solution.py:569
  84.6 1.6 %to_time.2.refs_5_ = bf16[320,1024]{1,0:T(8,128)(2,1)} custom-call(bf16[80,1024]{1,0:T(8,128)(2,1)S(1)} %add_convert_fusion.1.refs_0_, bf16[80,1024]{1,0:T(8,128)(2,1)S(1)} %add_convert_fusion.refs_1_, bf16[80,1024]{1,0:T(8,128)(2,1)S(1)} %collective-permute-done.20.refs_2_, bf16[80,1024]{1,0:T(8,128)(2,1)S(1)} %collective-permute-done.21.refs_3_, ...), custom_call_target="tpu_custom_call" | custom-call | flops 335544320 | bytes 2097152 | tf_op jit(solution)/shard_map/to_time/pallas_call | solution.py:372
  86.2 0.0 collective-permute-done.16.refs_2_
  86.2 0.2 collective-permute-done.17.refs_3_
  86.4 1.5 %to_time.3 = bf16[320,1024]{1,0:T(8,128)(2,1)} custom-call(bf16[80,1024]{1,0:T(8,128)(2,1)S(1)} %add_convert_fusion.3.refs_0_, bf16[80,1024]{1,0:T(8,128)(2,1)S(1)} %add_convert_fusion.2.refs_1_, bf16[80,1024]{1,0:T(8,128)(2,1)S(1)} %collective-permute-done.16.refs_2_, ...), custom_call_target="tpu_custom_call", output_to_operand_aliasing={{}: (5, {})} | custom-call | flops 335544320 | bytes 2097152 | tf_op jit(solution)/shard_map/to_time/pallas_call | solution.py:372
  (32 shorter events, 0.4 us)
Async XLA Ops:
  0.0 7.3 %copy-start = (bf16[320,1024]{1,0:T(8,128)(2,1)S(1)}, bf16[320,1024]{1,0:T(8,128)(2,1)}, u32[]{:S(2)}) copy-start(bf16[320,1024]{1,0:T(8,128)(2,1)} %param.5) | copy-start | bytes 1966084
  1.1 9.4 %copy-start.2 = (s32[1280]{0:T(1024)S(1)}, s32[1280]{0:T(1024)}, u32[]{:S(2)}) copy-start(s32[1280]{0:T(1024)} %param.6) | copy-start | bytes 15364
  1.1 9.6 %copy-start.1 = (s32[16,16]{1,0:T(8,128)S(1)}, s32[16,16]{1,0:T(8,128)}, u32[]{:S(2)}) copy-start(s32[16,16]{1,0:T(8,128)} %param.7) | copy-start | bytes 3076
  1.1 13.0 %collective-permute-start.1 = (bf16[160,1024]{1,0:T(8,128)(2,1)S(1)}, bf16[160,1024]{1,0:T(8,128)(2,1)S(1)}, u32[]{:S(2)}, u32[]{:S(2)}) collective-permute-start(bf16[160,1024]{1,0:T(8,128)(2,1)S(1)} %pad_maximum_fusion.refs_0_), channel_id=1, source_target_pairs={{0,4},{12,8},{1,5},{13,9},{2,6},{14,10},{3,7},{15,11},{16,20},{28,... | collective-permute-start | bytes 983048 | tf_op jit(solution)/shard_map/ppermute | solution.py:505
  7.4 23.0 %collective-permute-start = (bf16[160,1024]{1,0:T(8,128)(2,1)S(1)}, bf16[160,1024]{1,0:T(8,128)(2,1)S(1)}, u32[]{:S(2)}, u32[]{:S(2)}) collective-permute-start(bf16[160,1024]{1,0:T(8,128)(2,1)S(1)} %pad_maximum_fusion.1.refs_0_), channel_id=1, source_target_pairs={{0,4},{12,8},{1,5},{13,9},{2,6},{14,10},{3,7},{15,11},{16,20},{28,... | collective-permute-start | bytes 983048 | tf_op jit(solution)/shard_map/ppermute | solution.py:505
  8.7 19.5 %collective-permute-start.4 = (bf16[160,1024]{1,0:T(8,128)(2,1)S(1)}, bf16[160,1024]{1,0:T(8,128)(2,1)S(1)}, u32[]{:S(2)}, u32[]{:S(2)}) collective-permute-start(bf16[160,1024]{1,0:T(8,128)(2,1)S(1)} %pad_maximum_fusion.3.refs_1_), channel_id=1, source_target_pairs={{0,4},{12,8},{1,5},{13,9},{2,6},{14,10},{3,7},{15,11},{16,20},{28,... | collective-permute-start | bytes 983048 | tf_op jit(solution)/shard_map/ppermute | solution.py:505
  14.7 15.6 %collective-permute-start.2 = (bf16[160,1024]{1,0:T(8,128)(2,1)S(1)}, bf16[160,1024]{1,0:T(8,128)(2,1)S(1)}, u32[]{:S(2)}, u32[]{:S(2)}) collective-permute-start(bf16[160,1024]{1,0:T(8,128)(2,1)S(1)} %spectra.4.refs_0_), channel_id=1, source_target_pairs={{4,8},{8,4},{5,9},{9,5},{6,10},{10,6},{7,11},{11,7},{20,24},{24,20... | collective-permute-start | bytes 983048 | tf_op jit(solution)/shard_map/ppermute | solution.py:544
  15.4 18.7 %collective-permute-start.3 = (bf16[160,1024]{1,0:T(8,128)(2,1)S(1)}, bf16[160,1024]{1,0:T(8,128)(2,1)S(1)}, u32[]{:S(2)}, u32[]{:S(2)}) collective-permute-start(bf16[160,1024]{1,0:T(8,128)(2,1)S(1)} %pad_maximum_fusion.2.refs_1_), channel_id=1, source_target_pairs={{0,4},{12,8},{1,5},{13,9},{2,6},{14,10},{3,7},{15,11},{16,20},{28,... | collective-permute-start | bytes 983048 | tf_op jit(solution)/shard_map/ppermute | solution.py:505
  28.8 5.4 %collective-permute-start.5 = (bf16[160,1024]{1,0:T(8,128)(2,1)S(1)}, bf16[160,1024]{1,0:T(8,128)(2,1)S(1)}, u32[]{:S(2)}, u32[]{:S(2)}) collective-permute-start(bf16[160,1024]{1,0:T(8,128)(2,1)S(1)} %spectra.6.refs_2_), channel_id=1, source_target_pairs={{4,8},{8,4},{5,9},{9,5},{6,10},{10,6},{7,11},{11,7},{20,24},{24,20... | collective-permute-start | bytes 983048 | tf_op jit(solution)/shard_map/ppermute | solution.py:544
  30.9 5.9 %collective-permute-start.12 = (bf16[160,1024]{1,0:T(8,128)(2,1)S(1)}, bf16[160,1024]{1,0:T(8,128)(2,1)S(1)}, u32[]{:S(2)}, u32[]{:S(2)}) collective-permute-start(bf16[160,1024]{1,0:T(8,128)(2,1)S(1)} %get-tuple-element.44), channel_id=1, source_target_pairs={{4,8},{8,4},{5,9},{9,5},{6,10},{10,6},{7,11},{11,7},{20,24},{24,20... | collective-permute-start | bytes 983048 | tf_op jit(solution)/shard_map/ppermute | solution.py:556
  31.6 10.3 %collective-permute-start.9 = (bf16[160,1024]{1,0:T(8,128)(2,1)S(1)}, bf16[160,1024]{1,0:T(8,128)(2,1)S(1)}, u32[]{:S(2)}, u32[]{:S(2)}) collective-permute-start(bf16[160,1024]{1,0:T(8,128)(2,1)S(1)} %get-tuple-element.36.refs_0_.refs_2_.refs_4_), channel_id=1, source_target_pairs={{0,2},{2,0},{1,3},{3,1},{4,6},{6,4},{5,7},{7,5},{8,10},{10,8},{9,1... | collective-permute-start | bytes 983048 | tf_op jit(solution)/shard_map/ppermute | solution.py:24
  34.7 11.4 %collective-permute-start.6 = (bf16[160,1024]{1,0:T(8,128)(2,1)S(1)}, bf16[160,1024]{1,0:T(8,128)(2,1)S(1)}, u32[]{:S(2)}, u32[]{:S(2)}) collective-permute-start(bf16[160,1024]{1,0:T(8,128)(2,1)S(1)} %get-tuple-element.39.refs_1_.refs_6_.refs_8_), channel_id=1, source_target_pairs={{0,2},{2,0},{1,3},{3,1},{4,6},{6,4},{5,7},{7,5},{8,10},{10,8},{9,1... | collective-permute-start | bytes 983048 | tf_op jit(solution)/shard_map/ppermute | solution.py:24
  36.2 9.9 %collective-permute-start.8 = (bf16[160,1024]{1,0:T(8,128)(2,1)S(1)}, bf16[160,1024]{1,0:T(8,128)(2,1)S(1)}, u32[]{:S(2)}, u32[]{:S(2)}) collective-permute-start(bf16[160,1024]{1,0:T(8,128)(2,1)S(1)} %get-tuple-element.36.refs_0_.refs_2_.refs_4_), channel_id=1, source_target_pairs={{0,1},{1,0},{2,3},{3,2},{4,5},{5,4},{6,7},{7,6},{8,9},{9,8},{10,11... | collective-permute-start | bytes 983048 | tf_op jit(solution)/shard_map/ppermute | solution.py:24
  36.2 9.9 %collective-permute-start.11 = (bf16[160,1024]{1,0:T(8,128)(2,1)S(1)}, bf16[160,1024]{1,0:T(8,128)(2,1)S(1)}, u32[]{:S(2)}, u32[]{:S(2)}) collective-permute-start(bf16[160,1024]{1,0:T(8,128)(2,1)S(1)} %get-tuple-element.39.refs_1_.refs_6_.refs_8_), channel_id=1, source_target_pairs={{0,1},{1,0},{2,3},{3,2},{4,5},{5,4},{6,7},{7,6},{8,9},{9,8},{10,11... | collective-permute-start | bytes 983048 | tf_op jit(solution)/shard_map/ppermute | solution.py:24
  36.7 9.4 %collective-permute-start.13 = (bf16[160,1024]{1,0:T(8,128)(2,1)S(1)}, bf16[160,1024]{1,0:T(8,128)(2,1)S(1)}, u32[]{:S(2)}, u32[]{:S(2)}) collective-permute-start(bf16[160,1024]{1,0:T(8,128)(2,1)S(1)} %get-tuple-element.45), channel_id=1, source_target_pairs={{4,8},{8,4},{5,9},{9,5},{6,10},{10,6},{7,11},{11,7},{20,24},{24,20... | collective-permute-start | bytes 983048 | tf_op jit(solution)/shard_map/ppermute | solution.py:556
  41.9 4.3 %collective-permute-start.10 = (bf16[160,1024]{1,0:T(8,128)(2,1)S(1)}, bf16[160,1024]{1,0:T(8,128)(2,1)S(1)}, u32[]{:S(2)}, u32[]{:S(2)}) collective-permute-start(bf16[160,1024]{1,0:T(8,128)(2,1)S(1)} %collective-permute-done.9.refs_4_.refs_6_), channel_id=1, source_target_pairs={{0,1},{1,0},{2,3},{3,2},{4,5},{5,4},{6,7},{7,6},{8,9},{9,8},{10,11... | collective-permute-start | bytes 983048 | tf_op jit(solution)/shard_map/ppermute | solution.py:24
  46.1 1.6 %collective-permute-start.7 = (bf16[160,1024]{1,0:T(8,128)(2,1)S(1)}, bf16[160,1024]{1,0:T(8,128)(2,1)S(1)}, u32[]{:S(2)}, u32[]{:S(2)}) collective-permute-start(bf16[160,1024]{1,0:T(8,128)(2,1)S(1)} %collective-permute-done.6.refs_2_.refs_10_), channel_id=1, source_target_pairs={{0,1},{1,0},{2,3},{3,2},{4,5},{5,4},{6,7},{7,6},{8,9},{9,8},{10,11... | collective-permute-start | bytes 983048 | tf_op jit(solution)/shard_map/ppermute | solution.py:24
  49.3 4.6 %collective-permute-start.14 = (bf16[80,1024]{1,0:T(8,128)(2,1)S(1)}, bf16[80,1024]{1,0:T(8,128)(2,1)S(1)}, u32[]{:S(2)}, u32[]{:S(2)}) collective-permute-start(bf16[80,1024]{1,0:T(8,128)(2,1)S(1)} %get-tuple-element.48), channel_id=1, source_target_pairs={{4,8},{8,4},{5,9},{9,5},{6,10},{10,6},{7,11},{11,7},{20,24},{24,20... | collective-permute-start | bytes 491528 | tf_op jit(solution)/shard_map/ppermute | solution.py:566
  49.9 8.0 %collective-permute-start.15 = (bf16[80,1024]{1,0:T(8,128)(2,1)S(1)}, bf16[80,1024]{1,0:T(8,128)(2,1)S(1)}, u32[]{:S(2)}, u32[]{:S(2)}) collective-permute-start(bf16[80,1024]{1,0:T(8,128)(2,1)S(1)} %get-tuple-element.50), channel_id=1, source_target_pairs={{4,8},{8,4},{5,9},{9,5},{6,10},{10,6},{7,11},{11,7},{20,24},{24,20... | collective-permute-start | bytes 491528 | tf_op jit(solution)/shard_map/ppermute | solution.py:566
  52.5 2.7 %collective-permute-start.18 = (bf16[80,1024]{1,0:T(8,128)(2,1)S(1)}, bf16[80,1024]{1,0:T(8,128)(2,1)S(1)}, u32[]{:S(2)}, u32[]{:S(2)}) collective-permute-start(bf16[80,1024]{1,0:T(8,128)(2,1)S(1)} %get-tuple-element.43), channel_id=1, source_target_pairs={{4,8},{8,4},{5,9},{9,5},{6,10},{10,6},{7,11},{11,7},{20,24},{24,20... | collective-permute-start | bytes 491528 | tf_op jit(solution)/shard_map/ppermute | solution.py:566
  53.2 3.4 %collective-permute-start.19 = (bf16[80,1024]{1,0:T(8,128)(2,1)S(1)}, bf16[80,1024]{1,0:T(8,128)(2,1)S(1)}, u32[]{:S(2)}, u32[]{:S(2)}) collective-permute-start(bf16[80,1024]{1,0:T(8,128)(2,1)S(1)} %get-tuple-element.49), channel_id=1, source_target_pairs={{4,8},{8,4},{5,9},{9,5},{6,10},{10,6},{7,11},{11,7},{20,24},{24,20... | collective-permute-start | bytes 491528 | tf_op jit(solution)/shard_map/ppermute | solution.py:566
  53.9 32.2 %collective-permute-start.16 = (bf16[80,1024]{1,0:T(8,128)(2,1)S(1)}, bf16[80,1024]{1,0:T(8,128)(2,1)S(1)}, u32[]{:S(2)}, u32[]{:S(2)}) collective-permute-start(bf16[80,1024]{1,0:T(8,128)(2,1)S(1)} %add_convert_fusion.3.refs_0_), channel_id=1, source_target_pairs={{4,0},{8,12},{5,1},{9,13},{6,2},{10,14},{7,3},{11,15},{20,16},{24,... | collective-permute-start | bytes 491528 | tf_op jit(solution)/shard_map/ppermute | solution.py:569
  55.3 26.7 %collective-permute-start.20 = (bf16[80,1024]{1,0:T(8,128)(2,1)S(1)}, bf16[80,1024]{1,0:T(8,128)(2,1)S(1)}, u32[]{:S(2)}, u32[]{:S(2)}) collective-permute-start(bf16[80,1024]{1,0:T(8,128)(2,1)S(1)} %add_convert_fusion.1.refs_0_), channel_id=1, source_target_pairs={{4,0},{8,12},{5,1},{9,13},{6,2},{10,14},{7,3},{11,15},{20,16},{24,... | collective-permute-start | bytes 491528 | tf_op jit(solution)/shard_map/ppermute | solution.py:569
  56.7 27.9 %collective-permute-start.21 = (bf16[80,1024]{1,0:T(8,128)(2,1)S(1)}, bf16[80,1024]{1,0:T(8,128)(2,1)S(1)}, u32[]{:S(2)}, u32[]{:S(2)}) collective-permute-start(bf16[80,1024]{1,0:T(8,128)(2,1)S(1)} %add_convert_fusion.refs_1_), channel_id=1, source_target_pairs={{4,0},{8,12},{5,1},{9,13},{6,2},{10,14},{7,3},{11,15},{20,16},{24,... | collective-permute-start | bytes 491528 | tf_op jit(solution)/shard_map/ppermute | solution.py:569
  58.0 28.3 %collective-permute-start.17 = (bf16[80,1024]{1,0:T(8,128)(2,1)S(1)}, bf16[80,1024]{1,0:T(8,128)(2,1)S(1)}, u32[]{:S(2)}, u32[]{:S(2)}) collective-permute-start(bf16[80,1024]{1,0:T(8,128)(2,1)S(1)} %add_convert_fusion.2.refs_1_), channel_id=1, source_target_pairs={{4,0},{8,12},{5,1},{9,13},{6,2},{10,14},{7,3},{11,15},{20,16},{24,... | collective-permute-start | bytes 491528 | tf_op jit(solution)/shard_map/ppermute | solution.py:569
where the time goes:
time: 88.4 us; the launch traced here: 87.9 us
  waiting for transfers between devices  42.4 us (48%)
  starting transfers between devices  29 us (33%)
  Pallas kernels  11.6 us (13%)
  local copies, waits for them, and re-layouts  2.93 us (3%)
  other arithmetic  1.32 us (1%)
    ppermute x4, waiting for transfers between devices, finish(): arrived.append(lax.ppermute(sums[-1], 'blk', outward))  25.5 us
    ppermute x4, starting transfers between devices, inner_body(): arrived.append(lax.ppermute(block, 'blk', inward))  14.8 us
    ppermute x6, waiting for transfers between devices, shift(): return lax.ppermute(value, axis, pairs)  10.3 us
    ppermute x4, waiting for transfers between devices, inner_body(): arrived.append(lax.ppermute(block, 'blk', inward))  6.64 us
    ppermute x4, starting transfers between devices, finish(): arrived.append(lax.ppermute(sums[-1], 'blk', outward))  5.17 us
    ppermute x6, starting transfers between devices, shift(): return lax.ppermute(value, axis, pairs)  3.6 us
    pallas_call x3, Pallas kernels, couple(): pl.pallas_call(functools.partial(couple_kernel, piece, len(rows), len(col...  3.38 us
    pallas_call x2, Pallas kernels, to_time(): pl.pallas_call(functools.partial(to_time_kernel, len(here), own_side), in...  3.1 us
  transfers between devices with their start and end apart: 22, of which 8 were waited for; matrix products, arithmetic and copies ran while one was open for 4% of the time, Pallas kernels for 10%

commit v1 on v0

--- a/solution.py
+++ b/solution.py
@@ -343,8 +343,8 @@
     copies = []
     for part in range(2):
         columns = slice(part * wide, (part + 1) * wide)
-        traces = lax.dot_general(
-            adjoint, basis_ref[columns, :], CONTRACT_LAST, preferred_element_type=jnp.float32
+        traces = jnp.dot(
+            adjoint, basis_ref[:, columns], preferred_element_type=jnp.float32
         )
         stage_ref[:, columns] = (traces * (1.0 / math.sqrt(NF))).astype(jnp.bfloat16)
         copies.append(
@@ -360,7 +360,7 @@
 
 
 def to_time(own_side, here, there, basis, rows, before):
-    span = basis.shape[0]
+    span = basis.shape[1]
     half = sum(block.shape[0] for block in here)
     args = [*here, *there, basis]
     specs = [VMEM] * len(args)
@@ -413,6 +413,24 @@
         ),
         name="two_bases",
     )(*tables)
+
+
+def turn_kernel(basis_ref, out_ref):
+    out_ref[...] = basis_ref[...].T
+
+
+def turned(basis):
+    return pl.pallas_call(
+        turn_kernel,
+        in_specs=[VMEM],
+        out_specs=VMEM,
+        out_shape=jax.ShapeDtypeStruct(basis.shape[::-1], basis.dtype),
+        compiler_params=pltpu.CompilerParams(vmem_limit_bytes=12 << 20),
+        cost_estimate=pl.CostEstimate(
+            flops=basis.size, bytes_accessed=4 * basis.size, transcendentals=0
+        ),
+        name="turned",
+    )(basis)
 
 
 def own_parts_kernel(count, *refs):
@@ -542,6 +560,8 @@
         (summed,) = spectra(passed_parts[place], near_passed[place], near_basis)
         to_pass.append(summed)
         kept_rest.append(lax.ppermute(summed, "blk", swapped))
+    turned_basis = turned(here_basis)
+    near_kept[0], turned_basis = lax.optimization_barrier((near_kept[0], turned_basis))
     own, passed_rest, cols = [], [], {}
     for place in range(per_half):
         whole, summed = spectra(
@@ -572,8 +592,8 @@
     first = finish(own_part, other_part)
     second = finish(other_part, own_part)
     rows = synthetic.shape[0]
-    traces = to_time(False, *first, here_basis, rows, None)
-    return to_time(True, *second, here_basis, rows, traces)
+    traces = to_time(False, *first, turned_basis, rows, None)
+    return to_time(True, *second, turned_basis, rows, traces)
 
 
 def shards(*args):

time: 88.4 us -> 87.7 us (level)
  transfers between devices with their start and end apart: 22 -> 22, of which waited for: 8 -> 9; matrix products, arithmetic and copies ran while one was open for 4% -> 4% of each run, Pallas kernels for 10% -> 10%
where the time goes in v1:
time: 87.7 us; the launch traced here: 87.2 us
  waiting for transfers between devices  41.8 us (48%)
  starting transfers between devices  29 us (33%)
  Pallas kernels  11.4 us (13%)
  local copies, waits for them, and re-layouts  2.93 us (3%)
  other arithmetic  1.32 us (2%)
    ppermute x4, waiting for transfers between devices, finish(): arrived.append(lax.ppermute(sums[-1], 'blk', outward))  24.9 us
    ppermute x4, starting transfers between devices, inner_body(): arrived.append(lax.ppermute(block, 'blk', inward))  14.8 us
    ppermute x6, waiting for transfers between devices, shift(): return lax.ppermute(value, axis, pairs)  10.9 us
    ppermute x4, waiting for transfers between devices, inner_body(): arrived.append(lax.ppermute(block, 'blk', inward))  6.02 us
    ppermute x4, starting transfers between devices, finish(): arrived.append(lax.ppermute(sums[-1], 'blk', outward))  5.17 us
    ppermute x6, starting transfers between devices, shift(): return lax.ppermute(value, axis, pairs)  3.63 us
    pallas_call x3, Pallas kernels, couple(): pl.pallas_call(functools.partial(couple_kernel, piece, len(rows), len(col...  3.37 us
    ppermute x4, starting transfers between devices, finish(): rest = lax.ppermute(sent[place], 'blk', swapped)  2.68 us
  transfers between devices with their start and end apart: 22, of which 9 were waited for; matrix products, arithmetic and copies ran while one was open for 4% of the time, Pallas kernels for 10%

profile of v1, /device:TPU:0, one launch (start us, length us, event | category | flops | bytes accessed | tf_op | source)
XLA Modules:
  0.0 87.2 jit_solution(5144874288508064731)
XLA Ops:
  0.0 1.1 %constant_dynamic-slice_fusion.8 = (bf16[80,1024]{1,0:T(8,128)(2,1)S(1)}, bf16[80,1024]{1,0:T(8,128)(2,1)S(1)}) fusion(bf16[320,1024]{1,0:T(8,128)(2,1)} %param.5, s32[]{:T(128)S(6)} %select_n.133, bf16[320,1024]{1,0:T(8,128)(2,1)} %param.4), kind=kLoop, calls=%fused_computation.52 | loop fusion | bytes 655364 | tf_op jit(solution)/shard_map/dynamic_slice | solution.py:509
  1.1 0.0 copy-start.2
  1.1 0.0 copy-start.1
  1.1 5.0 %collective-permute-start.1 = (bf16[160,1024]{1,0:T(8,128)(2,1)S(1)}, bf16[160,1024]{1,0:T(8,128)(2,1)S(1)}, u32[]{:S(2)}, u32[]{:S(2)}) collective-permute-start(bf16[160,1024]{1,0:T(8,128)(2,1)S(1)} %pad_maximum_fusion.refs_0_), channel_id=1, source_target_pairs={{0,4},{12,8},{1,5},{13,9},{2,6},{14,10},{3,7},{15,11},{16,20},{28,... | collective-permute-start | bytes 983048 | tf_op jit(solution)/shard_map/ppermute | solution.py:523
  6.2 1.1 %constant_dynamic-slice_fusion.5 = (bf16[80,1024]{1,0:T(8,128)(2,1)S(1)}, bf16[80,1024]{1,0:T(8,128)(2,1)S(1)}, bf16[80,1024]{1,0:T(8,128)(2,1)S(1)}) fusion(bf16[320,1024]{1,0:T(8,128)(2,1)} %param.4, s32[]{:T(128)S(6)} %select_n.135, s32[]{:T(128)S(6)} %select_n.159, s32[]{:T(128)S(6)} %select_n.134), kind=kLoop, calls=%fused_computation.49 | loop fusion | bytes 983052 | tf_op jit(solution)/shard_map/dynamic_slice | solution.py:509
  7.4 1.3 %collective-permute-start = (bf16[160,1024]{1,0:T(8,128)(2,1)S(1)}, bf16[160,1024]{1,0:T(8,128)(2,1)S(1)}, u32[]{:S(2)}, u32[]{:S(2)}) collective-permute-start(bf16[160,1024]{1,0:T(8,128)(2,1)S(1)} %pad_maximum_fusion.1.refs_0_), channel_id=1, source_target_pairs={{0,4},{12,8},{1,5},{13,9},{2,6},{14,10},{3,7},{15,11},{16,20},{28,... | collective-permute-start | bytes 983048 | tf_op jit(solution)/shard_map/ppermute | solution.py:523
  8.7 1.3 %collective-permute-start.4 = (bf16[160,1024]{1,0:T(8,128)(2,1)S(1)}, bf16[160,1024]{1,0:T(8,128)(2,1)S(1)}, u32[]{:S(2)}, u32[]{:S(2)}) collective-permute-start(bf16[160,1024]{1,0:T(8,128)(2,1)S(1)} %pad_maximum_fusion.3.refs_1_), channel_id=1, source_target_pairs={{0,4},{12,8},{1,5},{13,9},{2,6},{14,10},{3,7},{15,11},{16,20},{28,... | collective-permute-start | bytes 983048 | tf_op jit(solution)/shard_map/ppermute | solution.py:523
  10.2 0.1 stack.35
  10.3 0.1 broadcast_in_dim.41
  10.4 0.1 eq.42
  10.5 0.1 fusion.21
  10.7 0.1 concatenate.25
  10.8 0.1 copy.7
  10.9 0.1 select_reduce_fusion
  11.0 0.1 slice.13.refs_6_
  11.1 0.1 fusion.22
  11.2 0.5 fusion.6
  11.7 0.3 fusion.14
  12.0 1.2 %two_bases.1 = (bf16[1024,1024]{1,0:T(8,128)(2,1)S(1)}, bf16[1024,1024]{1,0:T(8,128)(2,1)S(1)}) custom-call(f32[16,512]{1,0:T(8,128)S(1)} %get-tuple-element.79.refs_0_, f32[16,512]{1,0:T(8,128)S(1)} %get-tuple-element.80.refs_1_, f32[16,512]{1,0:T(8,128)S(1)} %get-tuple-element.74.refs_2_, f32[16,512]{1,0:T(8,128)S(1)} %get-tuple-element.73.refs_3_, ...), custom_call_target="tpu_custom_call" | custom-call | flops 8388608 | bytes 4194304 | tf_op jit(solution)/shard_map/two_bases/pallas_call | solution.py:404
  13.3 0.8 own_parts.3
  14.1 0.1 collective-permute-done.1.near_ref
  14.2 0.5 spectra.4.refs_0_
  14.7 0.7 collective-permute-start.2
  15.4 7.2 %collective-permute-start.3 = (bf16[160,1024]{1,0:T(8,128)(2,1)S(1)}, bf16[160,1024]{1,0:T(8,128)(2,1)S(1)}, u32[]{:S(2)}, u32[]{:S(2)}) collective-permute-start(bf16[160,1024]{1,0:T(8,128)(2,1)S(1)} %pad_maximum_fusion.2.refs_1_), channel_id=1, source_target_pairs={{0,4},{12,8},{1,5},{13,9},{2,6},{14,10},{3,7},{15,11},{16,20},{28,... | collective-permute-start | bytes 983048 | tf_op jit(solution)/shard_map/ppermute | solution.py:523
  22.6 5.6 %collective-permute-done.4.near_ref = bf16[160,1024]{1,0:T(8,128)(2,1)S(1)} collective-permute-done((bf16[160,1024]{1,0:T(8,128)(2,1)S(1)}, bf16[160,1024]{1,0:T(8,128)(2,1)S(1)}, u32[]{:S(2)}, u32[]{:S(2)}) %collective-permute-start.4) | collective-permute-done | bytes 327712 | tf_op jit(solution)/shard_map/ppermute | solution.py:523
  28.2 0.5 spectra.6.refs_2_
  28.8 0.7 collective-permute-start.5
  29.4 0.6 turned.1.refs_4_
  30.1 0.9 own_parts.2
  31.0 0.5 spectra.5
  31.5 0.7 collective-permute-start.12
  32.2 1.6 %collective-permute-start.9 = (bf16[160,1024]{1,0:T(8,128)(2,1)S(1)}, bf16[160,1024]{1,0:T(8,128)(2,1)S(1)}, u32[]{:S(2)}, u32[]{:S(2)}) collective-permute-start(bf16[160,1024]{1,0:T(8,128)(2,1)S(1)} %get-tuple-element.39.refs_0_.refs_2_.refs_4_), channel_id=1, source_target_pairs={{0,2},{2,0},{1,3},{3,1},{4,6},{6,4},{5,7},{7,5},{8,10},{10,8},{9,1... | collective-permute-start | bytes 983048 | tf_op jit(solution)/shard_map/ppermute | solution.py:24
  33.8 0.4 collective-permute-done.3.near_ref
  34.1 0.5 spectra.7
  34.7 1.6 %collective-permute-start.6 = (bf16[160,1024]{1,0:T(8,128)(2,1)S(1)}, bf16[160,1024]{1,0:T(8,128)(2,1)S(1)}, u32[]{:S(2)}, u32[]{:S(2)}) collective-permute-start(bf16[160,1024]{1,0:T(8,128)(2,1)S(1)} %get-tuple-element.42.refs_1_.refs_6_.refs_8_), channel_id=1, source_target_pairs={{0,2},{2,0},{1,3},{3,1},{4,6},{6,4},{5,7},{7,5},{8,10},{10,8},{9,1... | collective-permute-start | bytes 983048 | tf_op jit(solution)/shard_map/ppermute | solution.py:24
  36.2 0.0 collective-permute-start.8
  36.2 0.5 collective-permute-start.11
  36.7 0.7 collective-permute-start.13
  37.4 5.4 %collective-permute-done.9.refs_4_.refs_6_ = bf16[160,1024]{1,0:T(8,128)(2,1)S(1)} collective-permute-done((bf16[160,1024]{1,0:T(8,128)(2,1)S(1)}, bf16[160,1024]{1,0:T(8,128)(2,1)S(1)}, u32[]{:S(2)}, u32[]{:S(2)}) %collective-permute-start.9) | collective-permute-done | bytes 327712 | tf_op jit(solution)/shard_map/ppermute | solution.py:24
  42.9 3.9 %collective-permute-done.6.refs_2_.refs_10_ = bf16[160,1024]{1,0:T(8,128)(2,1)S(1)} collective-permute-done((bf16[160,1024]{1,0:T(8,128)(2,1)S(1)}, bf16[160,1024]{1,0:T(8,128)(2,1)S(1)}, u32[]{:S(2)}, u32[]{:S(2)}) %collective-permute-start.6) | collective-permute-done | bytes 327712 | tf_op jit(solution)/shard_map/ppermute | solution.py:24
  46.8 0.0 collective-permute-done.8.refs_3_.refs_5_
  46.8 0.0 collective-permute-done.13.refs_3_
  46.8 0.0 collective-permute-done.11.refs_7_.refs_9_
  46.8 0.0 collective-permute-done.10.refs_5_.refs_7_
  46.8 1.6 %collective-permute-done.7.refs_3_.refs_11_ = bf16[160,1024]{1,0:T(8,128)(2,1)S(1)} collective-permute-done((bf16[160,1024]{1,0:T(8,128)(2,1)S(1)}, bf16[160,1024]{1,0:T(8,128)(2,1)S(1)}, u32[]{:S(2)}, u32[]{:S(2)}) %collective-permute-start.7) | collective-permute-done | bytes 327712 | tf_op jit(solution)/shard_map/ppermute | solution.py:24
  48.4 1.5 %couple.5 = (bf16[80,1024]{1,0:T(8,128)(2,1)S(1)}, bf16[80,1024]{1,0:T(8,128)(2,1)S(1)}) custom-call(bf16[160,1024]{1,0:T(8,128)(2,1)S(1)} %spectra.4.refs_0_, bf16[160,1024]{1,0:T(8,128)(2,1)S(1)} %collective-permute-done.12.refs_1_, bf16[160,1024]{1,0:T(8,128)(2,1)S(1)} %spectra.6.refs_2_, bf16[160,1024]{1,0:T(8,128)(2,1)S(1)} %collective-permute-done.13.refs_3_, ...), custom_call_target="tpu_custom_call" | custom-call | flops 629145600 | bytes 3276800 | tf_op jit(solution)/shard_map/couple/pallas_call | solution.py:309
  49.9 0.7 collective-permute-start.14
  50.6 0.7 collective-permute-start.15
  51.3 1.2 %couple.3.refs_4_ = f32[160,1024]{1,0:T(8,128)S(1)} custom-call(bf16[160,1024]{1,0:T(8,128)(2,1)S(1)} %get-tuple-element.39.refs_0_.refs_2_.refs_4_, bf16[160,1024]{1,0:T(8,128)(2,1)S(1)} %get-tuple-element.42.refs_1_.refs_6_.refs_8_, bf16[160,1024]{1,0:T(8,128)(2,1)S(1)} %get-tuple-element.39.refs_0_.refs_2_.refs_4_, ...), custom_call_target="tpu_custom_call" | custom-call | flops 471859200 | bytes 2621440 | tf_op jit(solution)/shard_map/couple/pallas_call | solution.py:309
  52.4 0.7 couple.4
  53.1 0.7 collective-permute-start.18
  53.8 0.7 collective-permute-start.19
  54.6 1.3 %collective-permute-start.16 = (bf16[80,1024]{1,0:T(8,128)(2,1)S(1)}, bf16[80,1024]{1,0:T(8,128)(2,1)S(1)}, u32[]{:S(2)}, u32[]{:S(2)}) collective-permute-start(bf16[80,1024]{1,0:T(8,128)(2,1)S(1)} %add_convert_fusion.3.refs_0_), channel_id=1, source_target_pairs={{4,0},{8,12},{5,1},{9,13},{6,2},{10,14},{7,3},{11,15},{20,16},{24,... | collective-permute-start | bytes 491528 | tf_op jit(solution)/shard_map/ppermute | solution.py:589
  55.9 0.0 collective-permute-done.18
  55.9 1.3 %collective-permute-start.20 = (bf16[80,1024]{1,0:T(8,128)(2,1)S(1)}, bf16[80,1024]{1,0:T(8,128)(2,1)S(1)}, u32[]{:S(2)}, u32[]{:S(2)}) collective-permute-start(bf16[80,1024]{1,0:T(8,128)(2,1)S(1)} %add_convert_fusion.1.refs_0_), channel_id=1, source_target_pairs={{4,0},{8,12},{5,1},{9,13},{6,2},{10,14},{7,3},{11,15},{20,16},{24,... | collective-permute-start | bytes 491528 | tf_op jit(solution)/shard_map/ppermute | solution.py:589
  57.2 0.0 collective-permute-done.19
  57.3 1.3 %collective-permute-start.21 = (bf16[80,1024]{1,0:T(8,128)(2,1)S(1)}, bf16[80,1024]{1,0:T(8,128)(2,1)S(1)}, u32[]{:S(2)}, u32[]{:S(2)}) collective-permute-start(bf16[80,1024]{1,0:T(8,128)(2,1)S(1)} %add_convert_fusion.refs_1_), channel_id=1, source_target_pairs={{4,0},{8,12},{5,1},{9,13},{6,2},{10,14},{7,3},{11,15},{20,16},{24,... | collective-permute-start | bytes 491528 | tf_op jit(solution)/shard_map/ppermute | solution.py:589
  58.6 0.0 collective-permute-done.15
  58.6 1.3 %collective-permute-start.17 = (bf16[80,1024]{1,0:T(8,128)(2,1)S(1)}, bf16[80,1024]{1,0:T(8,128)(2,1)S(1)}, u32[]{:S(2)}, u32[]{:S(2)}) collective-permute-start(bf16[80,1024]{1,0:T(8,128)(2,1)S(1)} %add_convert_fusion.2.refs_1_), channel_id=1, source_target_pairs={{4,0},{8,12},{5,1},{9,13},{6,2},{10,14},{7,3},{11,15},{20,16},{24,... | collective-permute-start | bytes 491528 | tf_op jit(solution)/shard_map/ppermute | solution.py:589
  59.9 21.5 %collective-permute-done.20.refs_2_ = bf16[80,1024]{1,0:T(8,128)(2,1)S(1)} collective-permute-done((bf16[80,1024]{1,0:T(8,128)(2,1)S(1)}, bf16[80,1024]{1,0:T(8,128)(2,1)S(1)}, u32[]{:S(2)}, u32[]{:S(2)}) %collective-permute-start.20) | collective-permute-done | bytes 163872 | tf_op jit(solution)/shard_map/ppermute | solution.py:589
  81.4 2.8 %collective-permute-done.21.refs_3_ = bf16[80,1024]{1,0:T(8,128)(2,1)S(1)} collective-permute-done((bf16[80,1024]{1,0:T(8,128)(2,1)S(1)}, bf16[80,1024]{1,0:T(8,128)(2,1)S(1)}, u32[]{:S(2)}, u32[]{:S(2)}) %collective-permute-start.21) | collective-permute-done | bytes 163872 | tf_op jit(solution)/shard_map/ppermute | solution.py:589
  84.3 1.2 %to_time.2.refs_5_ = bf16[320,1024]{1,0:T(8,128)(2,1)} custom-call(bf16[80,1024]{1,0:T(8,128)(2,1)S(1)} %add_convert_fusion.1.refs_0_, bf16[80,1024]{1,0:T(8,128)(2,1)S(1)} %add_convert_fusion.refs_1_, bf16[80,1024]{1,0:T(8,128)(2,1)S(1)} %collective-permute-done.20.refs_2_, bf16[80,1024]{1,0:T(8,128)(2,1)S(1)} %collective-permute-done.21.refs_3_, ...), custom_call_target="tpu_custom_call" | custom-call | flops 335544320 | bytes 2097152 | tf_op jit(solution)/shard_map/to_time/pallas_call | solution.py:372
  85.5 0.5 collective-permute-done.17.refs_3_
  86.0 1.2 %to_time.3 = bf16[320,1024]{1,0:T(8,128)(2,1)} custom-call(bf16[80,1024]{1,0:T(8,128)(2,1)S(1)} %add_convert_fusion.3.refs_0_, bf16[80,1024]{1,0:T(8,128)(2,1)S(1)} %add_convert_fusion.2.refs_1_, bf16[80,1024]{1,0:T(8,128)(2,1)S(1)} %collective-permute-done.16.refs_2_, ...), custom_call_target="tpu_custom_call", output_to_operand_aliasing={{}: (5, {})} | custom-call | flops 335544320 | bytes 2097152 | tf_op jit(solution)/shard_map/to_time/pallas_call | solution.py:372
  (33 shorter events, 0.4 us)
Async XLA Ops:
  0.0 7.3 %copy-start = (bf16[320,1024]{1,0:T(8,128)(2,1)S(1)}, bf16[320,1024]{1,0:T(8,128)(2,1)}, u32[]{:S(2)}) copy-start(bf16[320,1024]{1,0:T(8,128)(2,1)} %param.5) | copy-start | bytes 1966084
  1.1 9.4 %copy-start.2 = (s32[1280]{0:T(1024)S(1)}, s32[1280]{0:T(1024)}, u32[]{:S(2)}) copy-start(s32[1280]{0:T(1024)} %param.6) | copy-start | bytes 15364
  1.1 9.6 %copy-start.1 = (s32[16,16]{1,0:T(8,128)S(1)}, s32[16,16]{1,0:T(8,128)}, u32[]{:S(2)}) copy-start(s32[16,16]{1,0:T(8,128)} %param.7) | copy-start | bytes 3076
  1.1 13.0 %collective-permute-start.1 = (bf16[160,1024]{1,0:T(8,128)(2,1)S(1)}, bf16[160,1024]{1,0:T(8,128)(2,1)S(1)}, u32[]{:S(2)}, u32[]{:S(2)}) collective-permute-start(bf16[160,1024]{1,0:T(8,128)(2,1)S(1)} %pad_maximum_fusion.refs_0_), channel_id=1, source_target_pairs={{0,4},{12,8},{1,5},{13,9},{2,6},{14,10},{3,7},{15,11},{16,20},{28,... | collective-permute-start | bytes 983048 | tf_op jit(solution)/shard_map/ppermute | solution.py:523
  7.4 23.6 %collective-permute-start = (bf16[160,1024]{1,0:T(8,128)(2,1)S(1)}, bf16[160,1024]{1,0:T(8,128)(2,1)S(1)}, u32[]{:S(2)}, u32[]{:S(2)}) collective-permute-start(bf16[160,1024]{1,0:T(8,128)(2,1)S(1)} %pad_maximum_fusion.1.refs_0_), channel_id=1, source_target_pairs={{0,4},{12,8},{1,5},{13,9},{2,6},{14,10},{3,7},{15,11},{16,20},{28,... | collective-permute-start | bytes 983048 | tf_op jit(solution)/shard_map/ppermute | solution.py:523
  8.7 19.5 %collective-permute-start.4 = (bf16[160,1024]{1,0:T(8,128)(2,1)S(1)}, bf16[160,1024]{1,0:T(8,128)(2,1)S(1)}, u32[]{:S(2)}, u32[]{:S(2)}) collective-permute-start(bf16[160,1024]{1,0:T(8,128)(2,1)S(1)} %pad_maximum_fusion.3.refs_1_), channel_id=1, source_target_pairs={{0,4},{12,8},{1,5},{13,9},{2,6},{14,10},{3,7},{15,11},{16,20},{28,... | collective-permute-start | bytes 983048 | tf_op jit(solution)/shard_map/ppermute | solution.py:523
  14.7 16.3 %collective-permute-start.2 = (bf16[160,1024]{1,0:T(8,128)(2,1)S(1)}, bf16[160,1024]{1,0:T(8,128)(2,1)S(1)}, u32[]{:S(2)}, u32[]{:S(2)}) collective-permute-start(bf16[160,1024]{1,0:T(8,128)(2,1)S(1)} %spectra.4.refs_0_), channel_id=1, source_target_pairs={{4,8},{8,4},{5,9},{9,5},{6,10},{10,6},{7,11},{11,7},{20,24},{24,20... | collective-permute-start | bytes 983048 | tf_op jit(solution)/shard_map/ppermute | solution.py:562
  15.4 18.7 %collective-permute-start.3 = (bf16[160,1024]{1,0:T(8,128)(2,1)S(1)}, bf16[160,1024]{1,0:T(8,128)(2,1)S(1)}, u32[]{:S(2)}, u32[]{:S(2)}) collective-permute-start(bf16[160,1024]{1,0:T(8,128)(2,1)S(1)} %pad_maximum_fusion.2.refs_1_), channel_id=1, source_target_pairs={{0,4},{12,8},{1,5},{13,9},{2,6},{14,10},{3,7},{15,11},{16,20},{28,... | collective-permute-start | bytes 983048 | tf_op jit(solution)/shard_map/ppermute | solution.py:523
  28.8 5.4 %collective-permute-start.5 = (bf16[160,1024]{1,0:T(8,128)(2,1)S(1)}, bf16[160,1024]{1,0:T(8,128)(2,1)S(1)}, u32[]{:S(2)}, u32[]{:S(2)}) collective-permute-start(bf16[160,1024]{1,0:T(8,128)(2,1)S(1)} %spectra.6.refs_2_), channel_id=1, source_target_pairs={{4,8},{8,4},{5,9},{9,5},{6,10},{10,6},{7,11},{11,7},{20,24},{24,20... | collective-permute-start | bytes 983048 | tf_op jit(solution)/shard_map/ppermute | solution.py:562
  31.5 5.2 %collective-permute-start.12 = (bf16[160,1024]{1,0:T(8,128)(2,1)S(1)}, bf16[160,1024]{1,0:T(8,128)(2,1)S(1)}, u32[]{:S(2)}, u32[]{:S(2)}) collective-permute-start(bf16[160,1024]{1,0:T(8,128)(2,1)S(1)} %get-tuple-element.47), channel_id=1, source_target_pairs={{4,8},{8,4},{5,9},{9,5},{6,10},{10,6},{7,11},{11,7},{20,24},{24,20... | collective-permute-start | bytes 983048 | tf_op jit(solution)/shard_map/ppermute | solution.py:576
  32.2 10.6 %collective-permute-start.9 = (bf16[160,1024]{1,0:T(8,128)(2,1)S(1)}, bf16[160,1024]{1,0:T(8,128)(2,1)S(1)}, u32[]{:S(2)}, u32[]{:S(2)}) collective-permute-start(bf16[160,1024]{1,0:T(8,128)(2,1)S(1)} %get-tuple-element.39.refs_0_.refs_2_.refs_4_), channel_id=1, source_target_pairs={{0,2},{2,0},{1,3},{3,1},{4,6},{6,4},{5,7},{7,5},{8,10},{10,8},{9,1... | collective-permute-start | bytes 983048 | tf_op jit(solution)/shard_map/ppermute | solution.py:24
  34.7 12.1 %collective-permute-start.6 = (bf16[160,1024]{1,0:T(8,128)(2,1)S(1)}, bf16[160,1024]{1,0:T(8,128)(2,1)S(1)}, u32[]{:S(2)}, u32[]{:S(2)}) collective-permute-start(bf16[160,1024]{1,0:T(8,128)(2,1)S(1)} %get-tuple-element.42.refs_1_.refs_6_.refs_8_), channel_id=1, source_target_pairs={{0,2},{2,0},{1,3},{3,1},{4,6},{6,4},{5,7},{7,5},{8,10},{10,8},{9,1... | collective-permute-start | bytes 983048 | tf_op jit(solution)/shard_map/ppermute | solution.py:24
  36.2 10.5 %collective-permute-start.8 = (bf16[160,1024]{1,0:T(8,128)(2,1)S(1)}, bf16[160,1024]{1,0:T(8,128)(2,1)S(1)}, u32[]{:S(2)}, u32[]{:S(2)}) collective-permute-start(bf16[160,1024]{1,0:T(8,128)(2,1)S(1)} %get-tuple-element.39.refs_0_.refs_2_.refs_4_), channel_id=1, source_target_pairs={{0,1},{1,0},{2,3},{3,2},{4,5},{5,4},{6,7},{7,6},{8,9},{9,8},{10,11... | collective-permute-start | bytes 983048 | tf_op jit(solution)/shard_map/ppermute | solution.py:24
  36.2 10.5 %collective-permute-start.11 = (bf16[160,1024]{1,0:T(8,128)(2,1)S(1)}, bf16[160,1024]{1,0:T(8,128)(2,1)S(1)}, u32[]{:S(2)}, u32[]{:S(2)}) collective-permute-start(bf16[160,1024]{1,0:T(8,128)(2,1)S(1)} %get-tuple-element.42.refs_1_.refs_6_.refs_8_), channel_id=1, source_target_pairs={{0,1},{1,0},{2,3},{3,2},{4,5},{5,4},{6,7},{7,6},{8,9},{9,8},{10,11... | collective-permute-start | bytes 983048 | tf_op jit(solution)/shard_map/ppermute | solution.py:24
  36.7 10.0 %collective-permute-start.13 = (bf16[160,1024]{1,0:T(8,128)(2,1)S(1)}, bf16[160,1024]{1,0:T(8,128)(2,1)S(1)}, u32[]{:S(2)}, u32[]{:S(2)}) collective-permute-start(bf16[160,1024]{1,0:T(8,128)(2,1)S(1)} %get-tuple-element.48), channel_id=1, source_target_pairs={{4,8},{8,4},{5,9},{9,5},{6,10},{10,6},{7,11},{11,7},{20,24},{24,20... | collective-permute-start | bytes 983048 | tf_op jit(solution)/shard_map/ppermute | solution.py:576
  42.9 3.9 %collective-permute-start.10 = (bf16[160,1024]{1,0:T(8,128)(2,1)S(1)}, bf16[160,1024]{1,0:T(8,128)(2,1)S(1)}, u32[]{:S(2)}, u32[]{:S(2)}) collective-permute-start(bf16[160,1024]{1,0:T(8,128)(2,1)S(1)} %collective-permute-done.9.refs_4_.refs_6_), channel_id=1, source_target_pairs={{0,1},{1,0},{2,3},{3,2},{4,5},{5,4},{6,7},{7,6},{8,9},{9,8},{10,11... | collective-permute-start | bytes 983048 | tf_op jit(solution)/shard_map/ppermute | solution.py:24
  46.8 1.6 %collective-permute-start.7 = (bf16[160,1024]{1,0:T(8,128)(2,1)S(1)}, bf16[160,1024]{1,0:T(8,128)(2,1)S(1)}, u32[]{:S(2)}, u32[]{:S(2)}) collective-permute-start(bf16[160,1024]{1,0:T(8,128)(2,1)S(1)} %collective-permute-done.6.refs_2_.refs_10_), channel_id=1, source_target_pairs={{0,1},{1,0},{2,3},{3,2},{4,5},{5,4},{6,7},{7,6},{8,9},{9,8},{10,11... | collective-permute-start | bytes 983048 | tf_op jit(solution)/shard_map/ppermute | solution.py:24
  49.9 4.6 %collective-permute-start.14 = (bf16[80,1024]{1,0:T(8,128)(2,1)S(1)}, bf16[80,1024]{1,0:T(8,128)(2,1)S(1)}, u32[]{:S(2)}, u32[]{:S(2)}) collective-permute-start(bf16[80,1024]{1,0:T(8,128)(2,1)S(1)} %get-tuple-element.51), channel_id=1, source_target_pairs={{4,8},{8,4},{5,9},{9,5},{6,10},{10,6},{7,11},{11,7},{20,24},{24,20... | collective-permute-start | bytes 491528 | tf_op jit(solution)/shard_map/ppermute | solution.py:586
  50.6 8.0 %collective-permute-start.15 = (bf16[80,1024]{1,0:T(8,128)(2,1)S(1)}, bf16[80,1024]{1,0:T(8,128)(2,1)S(1)}, u32[]{:S(2)}, u32[]{:S(2)}) collective-permute-start(bf16[80,1024]{1,0:T(8,128)(2,1)S(1)} %get-tuple-element.53), channel_id=1, source_target_pairs={{4,8},{8,4},{5,9},{9,5},{6,10},{10,6},{7,11},{11,7},{20,24},{24,20... | collective-permute-start | bytes 491528 | tf_op jit(solution)/shard_map/ppermute | solution.py:586
  53.1 2.7 %collective-permute-start.18 = (bf16[80,1024]{1,0:T(8,128)(2,1)S(1)}, bf16[80,1024]{1,0:T(8,128)(2,1)S(1)}, u32[]{:S(2)}, u32[]{:S(2)}) collective-permute-start(bf16[80,1024]{1,0:T(8,128)(2,1)S(1)} %get-tuple-element.46), channel_id=1, source_target_pairs={{4,8},{8,4},{5,9},{9,5},{6,10},{10,6},{7,11},{11,7},{20,24},{24,20... | collective-permute-start | bytes 491528 | tf_op jit(solution)/shard_map/ppermute | solution.py:586
  53.8 3.4 %collective-permute-start.19 = (bf16[80,1024]{1,0:T(8,128)(2,1)S(1)}, bf16[80,1024]{1,0:T(8,128)(2,1)S(1)}, u32[]{:S(2)}, u32[]{:S(2)}) collective-permute-start(bf16[80,1024]{1,0:T(8,128)(2,1)S(1)} %get-tuple-element.52), channel_id=1, source_target_pairs={{4,8},{8,4},{5,9},{9,5},{6,10},{10,6},{7,11},{11,7},{20,24},{24,20... | collective-permute-start | bytes 491528 | tf_op jit(solution)/shard_map/ppermute | solution.py:586
  54.6 30.9 %collective-permute-start.16 = (bf16[80,1024]{1,0:T(8,128)(2,1)S(1)}, bf16[80,1024]{1,0:T(8,128)(2,1)S(1)}, u32[]{:S(2)}, u32[]{:S(2)}) collective-permute-start(bf16[80,1024]{1,0:T(8,128)(2,1)S(1)} %add_convert_fusion.3.refs_0_), channel_id=1, source_target_pairs={{4,0},{8,12},{5,1},{9,13},{6,2},{10,14},{7,3},{11,15},{20,16},{24,... | collective-permute-start | bytes 491528 | tf_op jit(solution)/shard_map/ppermute | solution.py:589
  55.9 25.5 %collective-permute-start.20 = (bf16[80,1024]{1,0:T(8,128)(2,1)S(1)}, bf16[80,1024]{1,0:T(8,128)(2,1)S(1)}, u32[]{:S(2)}, u32[]{:S(2)}) collective-permute-start(bf16[80,1024]{1,0:T(8,128)(2,1)S(1)} %add_convert_fusion.1.refs_0_), channel_id=1, source_target_pairs={{4,0},{8,12},{5,1},{9,13},{6,2},{10,14},{7,3},{11,15},{20,16},{24,... | collective-permute-start | bytes 491528 | tf_op jit(solution)/shard_map/ppermute | solution.py:589
  57.3 27.0 %collective-permute-start.21 = (bf16[80,1024]{1,0:T(8,128)(2,1)S(1)}, bf16[80,1024]{1,0:T(8,128)(2,1)S(1)}, u32[]{:S(2)}, u32[]{:S(2)}) collective-permute-start(bf16[80,1024]{1,0:T(8,128)(2,1)S(1)} %add_convert_fusion.refs_1_), channel_id=1, source_target_pairs={{4,0},{8,12},{5,1},{9,13},{6,2},{10,14},{7,3},{11,15},{20,16},{24,... | collective-permute-start | bytes 491528 | tf_op jit(solution)/shard_map/ppermute | solution.py:589
  58.6 27.4 %collective-permute-start.17 = (bf16[80,1024]{1,0:T(8,128)(2,1)S(1)}, bf16[80,1024]{1,0:T(8,128)(2,1)S(1)}, u32[]{:S(2)}, u32[]{:S(2)}) collective-permute-start(bf16[80,1024]{1,0:T(8,128)(2,1)S(1)} %add_convert_fusion.2.refs_1_), channel_id=1, source_target_pairs={{4,0},{8,12},{5,1},{9,13},{6,2},{10,14},{7,3},{11,15},{20,16},{24,... | collective-permute-start | bytes 491528 | tf_op jit(solution)/shard_map/ppermute | solution.py:589
